TPU v7x, 32 devices: a whole 2x2x4 slice. The times are simulated.
32 devices in a mesh: row: 2 (over x), col: 4 (over y, core), layer: 4 (over z).
Axes of the slice: x: 2, y: 2, z: 4, core: 2. Of those that a mesh axis runs over, the one named last changes fastest.
Arguments:
- object_field: float32 [2, 512, 1024], P(None, 'row', 'col'), may hold values from -6 to 6
- probe_modes: float32 [2, 4, 256, 256], replicated, may hold values from -6 to 6
- amplitudes: float32 [32, 256, 256], P(('row', 'col', 'layer')), may hold values from 0 to 4
- offsets: int32 [32, 2], P(('row', 'col', 'layer')), may hold values from 0 to 768, as said below
Outputs:
- new_object: float32 [2, 512, 1024], P(None, 'row', 'col')
Inputs may be any that keep to these rules, and one draw needn't show every extreme that they name: `offsets`: every patch lies inside the 512 x 1024 object. A position held by the device at tile (r, c) has its corner inside that tile: rows r * 256 to (r + 1) * 256 - 1 and columns c * 256 to (c + 1) * 256 - 1. On a device whose tile row is not the last, its first position's patch reaches into the next tile row.
All inputs are finite; a program needn't handle non-finite values.
Results may differ from a plain program's by a relative error of at most 0.0001.
Values sent between devices are 32-bit elements; how exact they have to be, the bound alone decides.
A program may use at most 64 MiB of HBM per device.

v0:
```python
import contextlib
import functools

import jax
import jax.numpy as jnp
import numpy as np
from jax import lax
from jax.experimental import pallas as pl
from jax.experimental.pallas import tpu as pltpu
from jax.sharding import PartitionSpec as P

SOFTEN = 0.05
DAMPING = 0.5
AXES = ("row", "col", "layer")
PARTS = 4
LEAD = 2
IN_ROWS = 32
OUT_ROWS = 16
LAG_IN = 3
LAG_CROSS = 3


def scope(name):
    return contextlib.nullcontext()


def place():
    return tuple(lax.axis_index(a) for a in AXES)


def send(src, dst, send_sem, recv_sem, device):
    return pltpu.make_async_remote_copy(
        src_ref=src,
        dst_ref=dst,
        send_sem=send_sem,
        recv_sem=recv_sem,
        device_id=device,
        device_id_type=pl.DeviceIdType.MESH,
    )


def greet(rows, cols, layers):
    r, c, l = place()
    barrier = pltpu.get_barrier_semaphore()

    def tell(device):
        pl.semaphore_signal(
            barrier, inc=1, device_id=device, device_id_type=pl.DeviceIdType.MESH
        )

    near = (
        (c > 0, (r, c - 1, l)),
        (c < cols - 1, (r, c + 1, l)),
        (r > 0, (r - 1, c, l)),
        (r < rows - 1, (r + 1, c, l)),
    )
    for there, device in near:
        pl.when(there)(functools.partial(tell, device))
    for d in range(1, layers):
        tell((r, c, lax.rem(l + d, layers)))
    count = layers - 1
    for there, _ in near:
        count += there.astype(jnp.int32)
    pl.semaphore_wait(barrier, count)


def split(x):
    high = x.astype(jnp.bfloat16)
    return high, (x - high.astype(jnp.float32)).astype(jnp.bfloat16)


def prod(left, right):
    def one(a, b):
        return jnp.dot(a, b, preferred_element_type=jnp.float32)

    return one(left[0], right[0]) + (one(left[0], right[1]) + one(left[1], right[0]))


def corner_of(offs, group, layer, side):
    r, c, _ = place()
    tile_row = r - (1 if group >= 2 else 0)
    tile_col = c - (group % 2)
    return offs[group, layer, 0, 0] - tile_row * side, offs[group, layer, 0, 1] - tile_col * side


def kernel(
    sizes,
    corner_hbm, obj_hbm, probe_hbm, amp_hbm, fwd_high_hbm, fwd_low_hbm, inv_high_hbm, inv_low_hbm,
    out,
    corner, obj, probe, amp, fwd_high, fwd_low, inv_high, inv_low, offs, corners,
    right, below, diag, rolled, lines, far, ratio, power, weight,
    terms, left, own, lower, upper, inbound, crossed,
    s_load, s_corner, s_off, r_off, s_pass, r_pass,
    s_right, r_right, s_below, r_below, s_share, r_share, s_diag, r_diag, s_diag2, r_diag2,
    s_left, r_left, s_down, r_down, s_in, r_in, s_cross, r_cross, s_res, r_res,
):
    rows, cols, layers = sizes
    side = obj.shape[1]
    modes = probe.shape[1]
    tall = side // PARTS
    pieces_in = side // IN_ROWS
    steps = side // OUT_ROWS
    r, c, l = place()
    has_right, has_left = c < cols - 1, c > 0
    has_below, has_above = r < rows - 1, r > 0
    half = layers // 2
    low_half = l < half
    is_hub = (l == half - 1) | (l == half)
    has_outer = (l > 0) & (l < layers - 1)
    inner = (r, c, l + jnp.where(low_half, 1, -1))
    outer = (r, c, l + jnp.where(low_half, -1, 1))
    odd = lax.rem(l, 2)
    partner = (r, c, l + 1 - 2 * odd)
    west, east = (r, c - 1, l), (r, c + 1, l)
    north, south = (r - 1, c, l), (r + 1, c, l)

    loads = [
        pltpu.make_async_copy(src, dst, s_load.at[i])
        for i, (src, dst) in enumerate(
            (
                (corner_hbm, corner),
                (obj_hbm, obj),
                (probe_hbm, probe),
                (fwd_high_hbm, fwd_high),
                (fwd_low_hbm, fwd_low),
                (amp_hbm, amp),
                (inv_high_hbm, inv_high),
                (inv_low_hbm, inv_low),
            )
        )
    ]
    for copy in loads:
        copy.start()
    with scope("greet"):
        greet(rows, cols, layers)
    with scope("load"):
        loads[1].wait()

    def chunk(k, size):
        return pl.ds(k * size, size)

    lefts = [
        send(
            obj.at[:, chunk(k, IN_ROWS)], right.at[:, chunk(k, IN_ROWS)],
            s_right.at[k], r_right.at[k], west,
        )
        for k in range(pieces_in)
    ]
    ups, shares, diags, diags2 = [], [], [], []
    for i in range(pieces_in // 2):
        mine, other = chunk(2 * i + odd, IN_ROWS), chunk(2 * i + 1 - odd, IN_ROWS)
        ups.append(send(obj.at[:, mine], below.at[:, mine], s_below.at[i], r_below.at[i], north))
        shares.append(
            send(below.at[:, mine], below.at[:, mine], s_share.at[i], r_share.at[i], partner)
        )
        diags.append(send(below.at[:, mine], diag.at[:, mine], s_diag.at[i], r_diag.at[i], west))
        diags2.append(
            send(below.at[:, other], diag.at[:, other], s_diag2.at[i], r_diag2.at[i], west)
        )
    for i in range(pieces_in // 2):
        pl.when(has_above)(ups[i].start)
    for k in range(pieces_in):
        pl.when(has_left)(lefts[k].start)
    loads[0].wait()
    at = lax.broadcasted_iota(jnp.int32, (1, 1, 128), 2)
    offs[0, pl.ds(l, 1)] = jnp.where(at == 0, corner[0, 0], corner[0, 1])
    mine = offs.at[0, pl.ds(l, 1)]
    around = [(d, lax.rem(l + d, layers)) for d in range(1, layers)]
    peers = [send(mine, mine, s_off.at[d], r_off.at[d], (r, c, p)) for d, p in around]
    for peer in peers:
        peer.start()
    down = corner[0, 0] - r * side
    over = corner[0, 1] - c * side
    loads[2].wait()

    def prepare(m):
        for h in range(2):
            rolled[h, m] = pltpu.roll(pltpu.roll(probe[h, m], down, 0), over, 1)

    def forward(i):
        @pl.when(has_below)
        def _():
            ups[i].wait_recv()
            shares[i].start()
            pl.when(has_left)(diags[i].start)

    def forward2(i):
        @pl.when(has_below)
        def _():
            shares[i].wait_recv()
            pl.when(has_left)(diags2[i].start)

    across = send(offs.at[0], offs.at[1], s_pass.at[0], r_pass.at[0], east)
    down0 = send(offs.at[0], offs.at[2], s_pass.at[1], r_pass.at[1], south)
    down1 = send(offs.at[1], offs.at[3], s_pass.at[2], r_pass.at[2], south)

    def weigh(groups):
        there = (None, has_left, has_above, has_left & has_above)
        wide = lax.broadcasted_iota(jnp.int32, (side, side), 1)
        deep = lax.broadcasted_iota(jnp.int32, (side, side), 0)
        for group in groups:

            def add(layer, carry, group=group):
                a, b = corner_of(corners, group, layer, side)
                window = pltpu.roll(pltpu.roll(power[...], a, 0), b, 1)
                keep = (deep < a) if group >= 2 else (deep >= a)
                keep &= (wide < b) if group % 2 else (wide >= b)
                weight[...] += jnp.where(keep, window, 0.0)
                return carry

            def all_layers(add=add):
                lax.fori_loop(0, layers, add, 0)

            if there[group] is None:
                all_layers()
            else:
                pl.when(there[group])(all_layers)

    def fetch():
        copy = pltpu.make_async_copy(offs, corners, s_corner)
        copy.start()
        copy.wait()

    with scope("prep0"):
        prepare(0)
    with scope("peers"):
        for peer in peers:
            peer.wait()
        pl.when(has_right)(across.start)
    with scope("prep1"):
        power[...] = jnp.zeros_like(power)
        for m in range(1, modes):
            prepare(m)
        for m in range(modes):
            power[...] += probe[0, m] * probe[0, m] + probe[1, m] * probe[1, m]
    with scope("fwd0"):
        forward(0)
    with scope("across"):
        pl.when(has_left)(across.wait_recv)

        @pl.when(jnp.logical_not(has_left))
        def _():
            offs[1] = jnp.zeros(offs.shape[1:], jnp.int32)

        @pl.when(has_below)
        def _():
            down0.start()
            pl.when(has_left)(down1.start)

    weight[...] = jnp.full_like(weight, DAMPING)
    for i in range(1, pieces_in // 2 + 1):
        with scope(f"fwd{i}"):
            if i < pieces_in // 2:
                forward(i)
            forward2(i - 1)
        if i == 1:

            @pl.when(jnp.logical_not(has_above))
            def _():
                with scope("fetch"):
                    offs[2] = jnp.zeros(offs.shape[1:], jnp.int32)
                    offs[3] = jnp.zeros(offs.shape[1:], jnp.int32)
                    fetch()

        if i in (2, 3):

            @pl.when(jnp.logical_not(has_above))
            def _(i=i):
                with scope("weight"):
                    weigh((i - 2,))

    @pl.when(jnp.logical_not(has_above))
    def _():
        weight[...] = 1.0 / weight[...]

    with scope("loads"):
        for copy in loads[3:]:
            copy.wait()
    fwd, inv = (fwd_high, fwd_low), (inv_high, inv_low)

    def last(x, table):
        return prod(split(x), (table[0][...], table[1][...]))

    def first(table, x):
        a = (table[0][:, :side], table[1][:, :side])
        b = (table[0][:, side:], table[1][:, side:])
        return prod(a, split(x[:, :side])) + prod(b, split(x[:, side:]))

    lane = lax.broadcasted_iota(jnp.int32, (tall, side), 1)
    line = lax.broadcasted_iota(jnp.int32, (tall, side), 0)
    per_part = tall // IN_ROWS

    for k in range(PARTS):
        part = chunk(k, tall)
        with scope(f"merge{k}"):
            high = line + k * tall < down
            for h in range(2):
                own[h, part] = obj[h, part]

            @pl.when(has_right)
            def _():
                for i in range(k * per_part, (k + 1) * per_part):
                    lefts[i].wait_recv()
                for h in range(2):
                    own[h, part] = jnp.where(lane < over, right[h, part], own[h, part])

            @pl.when(has_below)
            def _():
                for h in range(2):
                    own[h, part] = jnp.where(high & (lane >= over), below[h, part], own[h, part])

            @pl.when(has_below & has_right)
            def _():
                for i in range(k * per_part // 2, (k + 1) * per_part // 2):
                    diags[i].wait_recv()
                    diags2[i].wait_recv()
                for h in range(2):
                    own[h, part] = jnp.where(high & (lane < over), diag[h, part], own[h, part])

        with scope(f"first{k}"):
            patch = [own[h, part] for h in range(2)]
            waves = []
            for m in range(modes):
                real, imag = (rolled[h, m, part] for h in range(2))
                waves.append(
                    jnp.concatenate(
                        [real * patch[0] - imag * patch[1], real * patch[1] + imag * patch[0]],
                        axis=1,
                    )
                )
            spread = last(jnp.concatenate(waves, axis=0), fwd)
            for m in range(modes):
                lines[m, part] = spread[m * tall : (m + 1) * tall]

    ratio[...] = jnp.zeros_like(ratio)

    def columns(m, carry):
        spread = first(inv, lines[m])
        far[m] = spread
        ratio[...] += spread[:side] * spread[:side] + spread[side:] * spread[side:]
        return carry

    with scope("columns"):
        lax.fori_loop(0, modes, columns, 0)
    ratio[...] = amp[0] / (jnp.sqrt(ratio[...]) + SOFTEN)

    def back(m, carry):
        scale = ratio[...]
        fixed = jnp.concatenate([far[m, :side] * scale, far[m, side:] * scale], axis=1)
        x = first(fwd, fixed)
        lines[m] = jnp.concatenate([x[:side], x[side:]], axis=1)
        return carry

    with scope("back"):
        lax.fori_loop(0, modes, back, 0)

    @pl.when(has_above)
    def _():
        with scope("fetch"):
            down0.wait_recv()
            pl.when(has_left)(down1.wait_recv)

            @pl.when(jnp.logical_not(has_left))
            def _():
                offs[3] = jnp.zeros(offs.shape[1:], jnp.int32)

            fetch()

    left_down, left_over = corner_of(corners, 1, l, side)

    def flow(src, dst, sems, device):
        return [
            send(
                src.at[:, chunk(k, OUT_ROWS)], dst.at[:, chunk(k, OUT_ROWS)],
                sems[0].at[k], sems[1].at[k], device,
            )
            for k in range(steps)
        ]

    rights = flow(terms, left, (s_left, r_left), east)
    downs = flow(lower, upper, (s_down, r_down), south)
    inward = flow(own, inbound, (s_in, r_in), inner)
    swaps = flow(own, crossed, (s_cross, r_cross), inner)
    results = flow(out, out, (s_res, r_res), outer)
    per_tall = tall // OUT_ROWS

    def rows_back(k):
        part = chunk(k, tall)
        x = jnp.concatenate([lines[m, part] for m in range(modes)], axis=0)
        x = last(x, inv)
        sums = [jnp.zeros((tall, side), jnp.float32)] * 2
        for m in range(modes):
            new_real = x[m * tall : (m + 1) * tall, :side]
            new_imag = x[m * tall : (m + 1) * tall, side:]
            real, imag = (rolled[h, m, part] for h in range(2))
            sums[0] += real * new_real + imag * new_imag
            sums[1] += real * new_imag - imag * new_real
        for h in range(2):
            terms[h, part] = sums[h]

        @pl.when(has_right)
        def _():
            for j in range(k * per_tall, (k + 1) * per_tall):
                rights[j].start()

    thin_lane = lax.broadcasted_iota(jnp.int32, (OUT_ROWS, side), 1)
    thin_line = lax.broadcasted_iota(jnp.int32, (OUT_ROWS, side), 0)

    def share_out(j):
        part = chunk(j, OUT_ROWS)
        at = thin_line + j * OUT_ROWS
        for h in range(2):
            mine = jnp.where(thin_lane >= over, terms[h, part], 0.0)
            own[h, part] = jnp.where(at >= down, mine, 0.0)
            lower[h, part] = jnp.where(at < down, mine, 0.0)

        @pl.when(has_left)
        def _():
            rights[j].wait_recv()
            for h in range(2):
                other = jnp.where(thin_lane < left_over, left[h, part], 0.0)
                own[h, part] += jnp.where(at >= left_down, other, 0.0)
                lower[h, part] += jnp.where(at < left_down, other, 0.0)

        pl.when(has_below)(downs[j].start)

    def enter(j):
        @pl.when(jnp.logical_not(has_outer))
        def _():
            if layers == 2:
                swaps[j].start()
            else:
                inward[j].start()

    def gather(j):
        part = chunk(j, OUT_ROWS)

        @pl.when(has_outer)
        def _():
            inward[j].wait_recv()
            for h in range(2):
                own[h, part] += inbound[h, part]
            pl.when(is_hub)(swaps[j].start)
            pl.when(jnp.logical_not(is_hub))(inward[j].start)

    def finish(j):
        part = chunk(j, OUT_ROWS)

        @pl.when(is_hub)
        def _():
            swaps[j].wait_recv()
            for h in range(2):
                number = own[h, part] + crossed[h, part] + DAMPING * obj[h, part]
                out[h, part] = number * weight[part]
            pl.when(has_outer)(results[j].start)

    def chain(s):
        if s < steps:
            enter(s)
        if LAG_IN <= s < steps + LAG_IN:
            gather(s - LAG_IN)
        if s >= LAG_IN + LAG_CROSS:
            finish(s - LAG_IN - LAG_CROSS)

    span = steps + LAG_IN + LAG_CROSS
    for k in range(LEAD):
        with scope(f"rb{k}"):
            rows_back(k)
    for s in range(span):
        if s % per_tall == 0 and s // per_tall + LEAD < PARTS:
            with scope(f"rb{s // per_tall + LEAD}"):
                rows_back(s // per_tall + LEAD)
        with scope(f"out{s}"):
            if s < steps:
                share_out(s)
            pl.when(jnp.logical_not(has_above))(functools.partial(chain, s))

    @pl.when(has_above)
    def _():
        with scope("weight"):
            weigh(range(4))
            weight[...] = 1.0 / weight[...]
        for s in range(span):
            with scope(f"chain{s}"):
                if s < steps:
                    part = chunk(s, OUT_ROWS)
                    downs[s].wait_recv()
                    for h in range(2):
                        own[h, part] += upper[h, part]
                chain(s)

    @pl.when(jnp.logical_not(is_hub))
    def _():
        for j in range(steps):
            with scope(f"res{j}"):
                results[j].wait_recv()
                pl.when(has_outer)(results[j].start)

    def sent(there, copies):
        @pl.when(there)
        def _():
            for copy in copies:
                copy.wait_send()

    with scope("drain"):
        sent(has_left, lefts)
        sent(has_above, ups)
        sent(has_below, shares + [down0])
        sent(has_below & has_left, diags + diags2 + [down1])
        sent(has_right, rights + [across])
        sent(has_below, downs)
        sent(jnp.logical_not(is_hub), inward)
        sent(is_hub, swaps)
        sent(has_outer, results)


def tables(side):
    steps = np.arange(side)
    angle = (steps[:, None] * steps[None, :] % side) * (2.0 * np.pi / side)
    real, imag = np.cos(angle) / np.sqrt(side), -np.sin(angle) / np.sqrt(side)
    both = np.block([[real, imag], [-imag, real]])

    def halves(x):
        x = x.astype(np.float32)
        high = x.astype(jnp.bfloat16)
        return high, (x - high.astype(np.float32)).astype(jnp.bfloat16)

    return halves(both) + halves(both.T)


def body(sizes, object_field, probe_modes, amplitudes, offsets):
    rows, cols, layers = sizes
    side = object_field.shape[1]
    assert object_field.shape[2] == side and probe_modes.shape[2] == side
    assert offsets.shape[0] == 1 and layers % 2 == 0
    assert side % (PARTS * 2 * IN_ROWS) == 0 and side % (PARTS * OUT_ROWS) == 0
    modes = probe_modes.shape[1]
    hbm = pl.BlockSpec(memory_space=pltpu.MemorySpace.HBM)
    vmem = pl.BlockSpec(memory_space=pltpu.MemorySpace.VMEM)
    pair = (2, side, side)
    f32 = jnp.float32
    dma = pltpu.SemaphoreType.DMA
    tabs = tuple(jnp.asarray(t) for t in tables(side))
    tab = pltpu.VMEM((2 * side, 2 * side), jnp.bfloat16)
    plane = pltpu.VMEM((side, side), f32)
    whole = pltpu.VMEM(pair, f32)
    corners = (4, layers, 1, 128)
    pieces_in, steps = side // IN_ROWS, side // OUT_ROWS
    return pl.pallas_call(
        functools.partial(kernel, sizes),
        out_shape=pltpu.VMEM(pair, f32),
        in_specs=[hbm] * 8,
        out_specs=vmem,
        scratch_shapes=[
            pltpu.SMEM((1, 2), jnp.int32),
            whole,
            pltpu.VMEM(probe_modes.shape, f32),
            pltpu.VMEM((1, side, side), f32),
        ]
        + [tab] * 4
        + [pltpu.VMEM(corners, jnp.int32), pltpu.SMEM(corners, jnp.int32)]
        + [whole] * 3
        + [
            pltpu.VMEM(probe_modes.shape, f32),
            pltpu.VMEM((modes, side, 2 * side), f32),
            pltpu.VMEM((modes, 2 * side, side), f32),
        ]
        + [plane] * 3
        + [whole] * 7
        + [dma((8,)), dma(())]
        + [dma((layers,))] * 2
        + [dma((3,))] * 2
        + [dma((pieces_in,))] * 2
        + [dma((pieces_in // 2,))] * 8
        + [dma((steps,))] * 10,
        compiler_params=pltpu.CompilerParams(
            collective_id=0, has_side_effects=True, vmem_limit_bytes=58 * 1024 * 1024
        ),
        name="update",
    )(offsets, object_field, probe_modes, amplitudes, *tabs)


def solution(mesh):
    sizes = tuple(mesh.shape[a] for a in AXES)
    placed = (
        P(None, "row", "col"),
        P(),
        P(("row", "col", "layer"), None, None),
        P(("row", "col", "layer"), None),
    )
    return jax.shard_map(
        functools.partial(body, sizes),
        mesh=mesh,
        in_specs=placed,
        out_specs=P(None, "row", "col"),
        check_vma=False,
    )
```

profile of v0, /device:TPU:6, one launch (start us, length us, event | category | flops | bytes accessed | tf_op | source)
XLA Modules:
  0.0 54.4 jit_solution(1894821630013780537)
XLA Ops:
  0.0 53.6 %update.1 = f32[2,256,256]{2,1,0:T(8,128)S(1)} custom-call(s32[1,2]{1,0:T(1,128)} %corner_hbm.1, f32[2,256,256]{2,1,0:T(8,128)} %obj_hbm.1, f32[2,4,256,256]{3,2,1,0:T(8,128)} %probe_hbm.1, f32[1,256,256]{2,1,0:T(8,128)} %amp_hbm.1, bf16[512,512]{1,0:T(8,128)(2,1)} %constant.8.clone.fwd_high_hbm, bf16[512,512]{1,0:T(8,128)(2,1)} %constant.9.clone.fwd_low_hbm, ...), custom_call_target="tpu_custom_call" | custom-call | tf_op jit(solution)/shard_map/update/pallas_call | solution.py:549
  53.6 0.8 %copy.10 = f32[2,256,256]{2,1,0:T(8,128)} copy(f32[2,256,256]{2,1,0:T(8,128)S(1)} %update.1) | data formatting | bytes 1048576
where the time goes:
time: 54.5 us; the launch traced here: 54.4 us
  Pallas kernels  53.6 us (98%)
  local copies, waits for them, and re-layouts  0.8 us (1%)
    pallas_call x1, Pallas kernels, body(): pl.pallas_call(functools.partial(kernel, sizes), out_shape=pltpu.VMEM(pai...  53.6 us

commit v1 on v0

v1 whole, which is shorter than its diff:
```python
import contextlib
import functools

import jax
import jax.numpy as jnp
import numpy as np
from jax import lax
from jax.experimental import pallas as pl
from jax.experimental.pallas import tpu as pltpu
from jax.sharding import PartitionSpec as P

SOFTEN = 0.05
DAMPING = 0.5
AXES = ("row", "col", "layer")
PARTS = 4
IN_ROWS = 16
UNROLL = 4
OUT_ROWS = 16
LAG_IN = 3
LAG_CROSS = 3


def scope(name):
    return contextlib.nullcontext()


def place():
    return tuple(lax.axis_index(a) for a in AXES)


def send(src, dst, send_sem, recv_sem, device):
    return pltpu.make_async_remote_copy(
        src_ref=src,
        dst_ref=dst,
        send_sem=send_sem,
        recv_sem=recv_sem,
        device_id=device,
        device_id_type=pl.DeviceIdType.MESH,
    )


def greet(rows, cols, layers):
    r, c, l = place()
    barrier = pltpu.get_barrier_semaphore()

    def tell(device):
        pl.semaphore_signal(
            barrier, inc=1, device_id=device, device_id_type=pl.DeviceIdType.MESH
        )

    near = (
        (c > 0, (r, c - 1, l)),
        (c < cols - 1, (r, c + 1, l)),
        (r > 0, (r - 1, c, l)),
        (r < rows - 1, (r + 1, c, l)),
    )
    for there, device in near:
        pl.when(there)(functools.partial(tell, device))
    for d in range(1, layers):
        tell((r, c, lax.rem(l + d, layers)))
    count = layers - 1
    for there, _ in near:
        count += there.astype(jnp.int32)
    pl.semaphore_wait(barrier, count)


def split(x):
    high = x.astype(jnp.bfloat16)
    return high, (x - high.astype(jnp.float32)).astype(jnp.bfloat16)


def prod(left, right):
    def one(a, b):
        return jnp.dot(a, b, preferred_element_type=jnp.float32)

    return one(left[0], right[0]) + (one(left[0], right[1]) + one(left[1], right[0]))


def corner_of(offs, group, layer, side):
    r, c, _ = place()
    tile_row = r - (1 if group >= 2 else 0)
    tile_col = c - (group % 2)
    return offs[group, layer, 0, 0] - tile_row * side, offs[group, layer, 0, 1] - tile_col * side


def kernel(
    sizes,
    corner_hbm, obj_hbm, probe_hbm, amp_hbm, fwd_high_hbm, fwd_low_hbm, inv_high_hbm, inv_low_hbm,
    out,
    corner, obj, probe, amp, fwd_high, fwd_low, inv_high, inv_low, offs, corners,
    right, below, diag, rolled, lines, far, ratio, power, weight,
    terms, left, own, lower, upper, inbound, crossed,
    s_load, s_corner, s_send, r_off, r_pass,
    r_right, r_below, r_share, r_diag, r_diag2, r_left, r_down, r_in, r_last,
):
    rows, cols, layers = sizes
    side = obj.shape[1]
    mid = side // 2
    modes = probe.shape[1]
    tall = side // PARTS
    pieces = side // IN_ROWS // 2
    steps = side // OUT_ROWS
    r, c, l = place()
    has_right, has_left = c < cols - 1, c > 0
    has_below, has_above = r < rows - 1, r > 0
    half = layers // 2
    low_half = l < half
    is_hub = (l == half - 1) | (l == half)
    has_outer = (l > 0) & (l < layers - 1)
    inner = (r, c, l + jnp.where(low_half, 1, -1))
    outer = (r, c, l + jnp.where(low_half, -1, 1))
    odd = lax.rem(l, 2)
    partner = (r, c, l + 1 - 2 * odd)
    west, east = (r, c - 1, l), (r, c + 1, l)
    north, south = (r - 1, c, l), (r + 1, c, l)
    odd_col = lax.rem(c, 2) == 1

    loads = [
        pltpu.make_async_copy(src, dst, s_load.at[i])
        for i, (src, dst) in enumerate(
            (
                (corner_hbm, corner),
                (obj_hbm, obj),
                (probe_hbm, probe),
                (amp_hbm, amp),
                (fwd_high_hbm, fwd_high),
                (fwd_low_hbm, fwd_low),
                (inv_high_hbm, inv_high),
                (inv_low_hbm, inv_low),
            )
        )
    ]
    for copy in loads:
        copy.start()
    with scope("greet"):
        greet(rows, cols, layers)
    with scope("load"):
        loads[1].wait()

    def chunk(k, size):
        return pl.ds(k * size, size)

    def piece(src, dst, part, send_sem, recv_sem, device):
        return send(src.at[:, part], dst.at[:, part], s_send.at[send_sem], recv_sem, device)

    lefts, lefts2, ups, shares, diags, diags2, extras = [], [], [], [], [], [], []
    for i in range(pieces):
        mine, other = chunk(2 * i + odd, IN_ROWS), chunk(2 * i + 1 - odd, IN_ROWS)
        lefts.append(piece(obj, right, mine, 0, r_right.at[i], west))
        lefts2.append(piece(obj, right, other, 0, r_right.at[pieces + i], west))
        ups.append(piece(obj, below, mine, 1, r_below.at[i], north))
        shares.append(piece(below, below, mine, 2, r_share.at[i], partner))
        diags.append(piece(below, diag, mine, 3, r_diag.at[i], west))
        diags2.append(piece(below, diag, other, 4, r_diag2.at[i], west))
        extras.append(piece(right, diag, other, 5, r_diag2.at[i], north))
    for copy in ups:
        pl.when(has_above)(copy.start)
    for copy in lefts2 + lefts:
        pl.when(has_left)(copy.start)
    with scope("load0"):
        loads[0].wait()
    at = lax.broadcasted_iota(jnp.int32, (1, 1, 128), 2)
    offs[0, pl.ds(l, 1)] = jnp.where(at == 0, corner[0, 0], corner[0, 1])
    mine = offs.at[0, pl.ds(l, 1)]
    around = [(d, lax.rem(l + d, layers)) for d in range(1, layers)]
    peers = [send(mine, mine, s_send.at[6], r_off.at[d - 1], (r, c, p)) for d, p in around]
    for peer in peers:
        peer.start()
    down = corner[0, 0] - r * side
    over = corner[0, 1] - c * side
    with scope("load2"):
        loads[2].wait()

    def prepare(m):
        for h in range(2):
            rolled[h, m] = pltpu.roll(pltpu.roll(probe[h, m], down, 0), over, 1)

    def forward(i):
        @pl.when(has_below)
        def _():
            ups[i].wait_recv()
            shares[i].start()
            pl.when(has_left)(diags[i].start)

        @pl.when(has_above & has_right & odd_col)
        def _():
            lefts2[i].wait_recv()
            extras[i].start()

    def forward2(i):
        @pl.when(has_below)
        def _():
            shares[i].wait_recv()
            pl.when(has_left & odd_col)(diags2[i].start)

    across = send(offs.at[0], offs.at[1], s_send.at[7], r_pass.at[0], east)
    down0 = send(offs.at[0], offs.at[2], s_send.at[8], r_pass.at[1], south)
    down1 = send(offs.at[1], offs.at[3], s_send.at[9], r_pass.at[2], south)

    def weigh(groups, first=0, last=layers):
        there = (None, has_left, has_above, has_left & has_above)
        wide = lax.broadcasted_iota(jnp.int32, (side, side), 1)
        deep = lax.broadcasted_iota(jnp.int32, (side, side), 0)
        for group in groups:

            def add(layer, carry, group=group):
                a, b = corner_of(corners, group, layer, side)
                window = pltpu.roll(pltpu.roll(power[...], a, 0), b, 1)
                keep = (deep < a) if group >= 2 else (deep >= a)
                keep &= (wide < b) if group % 2 else (wide >= b)
                weight[...] += jnp.where(keep, window, 0.0)
                return carry

            def all_layers(add=add):
                lax.fori_loop(first, last, add, 0)

            if there[group] is None:
                all_layers()
            else:
                pl.when(there[group])(all_layers)

    def fetch():
        copy = pltpu.make_async_copy(offs, corners, s_corner)
        copy.start()
        copy.wait()

    fetched = pltpu.make_async_copy(offs, corners, s_corner)

    with scope("prep"):
        for m in range(modes):
            prepare(m)
    with scope("amp"):
        power[...] = jnp.zeros_like(power)
        for m in range(modes):
            power[...] += probe[0, m] * probe[0, m] + probe[1, m] * probe[1, m]
        loads[3].wait()
        wide = lax.broadcasted_iota(jnp.int32, (side, side), 1)
        deep = lax.broadcasted_iota(jnp.int32, (side, side), 0)

        def pick(to, start):
            return to == jnp.where(start < mid, 2 * start, 2 * start - side + 1)

        turn = jnp.where(pick(wide, deep), 1.0, 0.0).astype(jnp.bfloat16)
        back_turn = jnp.where(pick(deep, wide), 1.0, 0.0).astype(jnp.bfloat16)

        def moved(x, along):
            total = None
            for _ in range(3):
                high = x.astype(jnp.bfloat16)
                x = x - high.astype(jnp.float32)
                pair = (turn, high) if along == 0 else (high, back_turn)
                one = jnp.dot(*pair, preferred_element_type=jnp.float32)
                total = one if total is None else total + one
            return total

        amp[0] = moved(moved(amp[0], 0), 1)
        weight[...] = jnp.full_like(weight, DAMPING)

    with scope("peers"):
        for peer in peers:
            peer.wait_recv()
        pl.when(has_right)(across.start)
    with scope("fwd0"):
        forward(0)
    for i in (1, 2):
        with scope(f"fwd{i}"):
            forward(i)
    with scope("across"):

        @pl.when(has_left)
        def _():
            across.wait_recv()

        @pl.when(jnp.logical_not(has_left))
        def _():
            offs[1] = jnp.zeros(offs.shape[1:], jnp.int32)

        @pl.when(has_below)
        def _():
            down0.start()
            pl.when(has_left)(down1.start)

        @pl.when(jnp.logical_not(has_above))
        def _():
            offs[2] = jnp.zeros(offs.shape[1:], jnp.int32)
            offs[3] = jnp.zeros(offs.shape[1:], jnp.int32)
            fetched.start()

    quarters = [(g, q * layers // 2, (q + 1) * layers // 2) for g in (0, 1) for q in range(2)]
    for i in range(3, pieces + 4):
        with scope(f"fwd{i}"):
            if i < pieces:
                forward(i)
            if i >= 4:
                forward2(i - 4)
        if 3 < i < 8:

            @pl.when(jnp.logical_not(has_above) & is_hub)
            def _(i=i):
                with scope(f"weight{i}"):
                    if i == 4:
                        fetched.wait()
                    group, start, stop = quarters[i - 4]
                    weigh((group,), start, stop)

    pl.when(jnp.logical_not(has_above | is_hub))(fetched.wait)

    with scope("loads"):
        for copy in loads[4:]:
            copy.wait()
    fwd, inv = (fwd_high, fwd_low), (inv_high, inv_low)

    def after(x, table, which):
        return prod(split(x), (table[0][which], table[1][which]))

    def ahead(table, which, x):
        return prod((table[0][which], table[1][which]), split(x))

    lane = lax.broadcasted_iota(jnp.int32, (tall, side), 1)
    line = lax.broadcasted_iota(jnp.int32, (tall, side), 0)
    per_part_in = tall // IN_ROWS // 2

    for k in range(PARTS):
        part = chunk(k, tall)
        with scope(f"merge{k}"):
            high = line + k * tall < down
            for h in range(2):
                own[h, part] = obj[h, part]

            @pl.when(has_right & jnp.logical_not(has_above & odd_col))
            def _():
                for i in range(k * per_part_in, (k + 1) * per_part_in):
                    lefts2[i].wait_recv()

            @pl.when(has_right)
            def _():
                for i in range(k * per_part_in, (k + 1) * per_part_in):
                    lefts[i].wait_recv()
                for h in range(2):
                    own[h, part] = jnp.where(lane < over, right[h, part], own[h, part])

            @pl.when(has_below)
            def _():
                for h in range(2):
                    own[h, part] = jnp.where(high & (lane >= over), below[h, part], own[h, part])

            @pl.when(has_below & has_right)
            def _():
                for i in range(k * per_part_in, (k + 1) * per_part_in):
                    diags[i].wait_recv()
                    diags2[i].wait_recv()
                for h in range(2):
                    own[h, part] = jnp.where(high & (lane < over), diag[h, part], own[h, part])

        with scope(f"first{k}"):
            patch = [own[h, part] for h in range(2)]
            sums, gaps = [], []
            for m in range(modes):
                real, imag = (rolled[h, m, part] for h in range(2))
                new = (real * patch[0] - imag * patch[1], real * patch[1] + imag * patch[0])
                sums.append(jnp.concatenate([x[:, :mid] + x[:, mid:] for x in new], axis=1))
                gaps.append(jnp.concatenate([x[:, :mid] - x[:, mid:] for x in new], axis=1))
            even = after(jnp.concatenate(sums, axis=0), fwd, 0)
            uneven = after(jnp.concatenate(gaps, axis=0), fwd, 1)
            for m in range(modes):
                here = slice(m * tall, (m + 1) * tall)
                for h in range(2):
                    there = slice(h * mid, (h + 1) * mid)
                    lines[m, h, part] = jnp.concatenate(
                        [even[here, there], uneven[here, there]], axis=1
                    )

    ratio[...] = jnp.zeros_like(ratio)

    def columns(m, carry):
        x = [lines[m, h] for h in range(2)]
        sums = jnp.concatenate([p[:mid] + p[mid:] for p in x], axis=0)
        gaps = jnp.concatenate([p[:mid] - p[mid:] for p in x], axis=0)
        for which, y in enumerate((sums, gaps)):
            spread = ahead(inv, which, y)
            far[m, which] = spread
            here = slice(which * mid, (which + 1) * mid)
            ratio[here] += spread[:mid] * spread[:mid] + spread[mid:] * spread[mid:]
        return carry

    with scope("columns"):
        lax.fori_loop(0, modes, columns, 0, unroll=UNROLL)
    ratio[...] = amp[0] / (jnp.sqrt(ratio[...]) + SOFTEN)

    def back(m, carry):
        turned = []
        for which in range(2):
            scale = ratio[which * mid : (which + 1) * mid]
            fixed = jnp.concatenate([far[m, which, :mid] * scale, far[m, which, mid:] * scale], axis=0)
            turned.append(ahead(fwd, which, fixed))
        total, gap = turned[0] + turned[1], turned[0] - turned[1]
        for h in range(2):
            there = slice(h * mid, (h + 1) * mid)
            lines[m, h, :mid] = total[there]
            lines[m, h, mid:] = gap[there]
        return carry

    with scope("back"):
        lax.fori_loop(0, modes, back, 0, unroll=UNROLL)

    @pl.when(has_above)
    def _():
        with scope("fetch"):
            down0.wait_recv()
            pl.when(has_left)(down1.wait_recv)

            @pl.when(jnp.logical_not(has_left))
            def _():
                offs[3] = jnp.zeros(offs.shape[1:], jnp.int32)

            fetched.start()
            fetched.wait()

    left_down, left_over = corner_of(corners, 1, l, side)

    def flow(src, dst, send_sem, recv_sem, device):
        return [
            piece(src, dst, chunk(k, OUT_ROWS), send_sem, recv_sem.at[k], device)
            for k in range(steps)
        ]

    rights = flow(terms, left, 10, r_left, east)
    downs = flow(lower, upper, 11, r_down, south)
    inward = flow(own, inbound, 12, r_in, inner)
    swaps = flow(own, crossed, 13, r_last, inner)
    results = flow(out, out, 14, r_last, outer)
    per_tall = tall // OUT_ROWS

    def rows_back(k):
        part = chunk(k, tall)
        both = []
        for which in range(2):
            here = slice(which * mid, (which + 1) * mid)
            x = [
                jnp.concatenate([lines[m, h, part, here] for h in range(2)], axis=1)
                for m in range(modes)
            ]
            both.append(after(jnp.concatenate(x, axis=0), inv, which))
        total, gap = both[0] + both[1], both[0] - both[1]
        sums = [jnp.zeros((tall, side), jnp.float32)] * 2
        for m in range(modes):
            here = slice(m * tall, (m + 1) * tall)
            new_real, new_imag = (
                jnp.concatenate(
                    [x[here, h * mid : (h + 1) * mid] for x in (total, gap)], axis=1
                )
                for h in range(2)
            )
            real, imag = (rolled[h, m, part] for h in range(2))
            sums[0] += real * new_real + imag * new_imag
            sums[1] += real * new_imag - imag * new_real
        for h in range(2):
            terms[h, part] = sums[h]

        @pl.when(has_right)
        def _():
            for j in range(k * per_tall, (k + 1) * per_tall):
                rights[j].start()

    thin_lane = lax.broadcasted_iota(jnp.int32, (OUT_ROWS, side), 1)
    thin_line = lax.broadcasted_iota(jnp.int32, (OUT_ROWS, side), 0)

    def share_out(j):
        part = chunk(j, OUT_ROWS)
        at = thin_line + j * OUT_ROWS
        for h in range(2):
            mine = jnp.where(thin_lane >= over, terms[h, part], 0.0)
            own[h, part] = jnp.where(at >= down, mine, 0.0)
            lower[h, part] = jnp.where(at < down, mine, 0.0)

        @pl.when(has_left)
        def _():
            rights[j].wait_recv()
            for h in range(2):
                other = jnp.where(thin_lane < left_over, left[h, part], 0.0)
                own[h, part] += jnp.where(at >= left_down, other, 0.0)
                lower[h, part] += jnp.where(at < left_down, other, 0.0)

        pl.when(has_below)(downs[j].start)

    def enter(j):
        @pl.when(jnp.logical_not(has_outer))
        def _():
            if layers == 2:
                swaps[j].start()
            else:
                inward[j].start()

    def gather(j):
        part = chunk(j, OUT_ROWS)

        @pl.when(has_outer)
        def _():
            inward[j].wait_recv()
            for h in range(2):
                own[h, part] += inbound[h, part]
            pl.when(is_hub)(swaps[j].start)
            pl.when(jnp.logical_not(is_hub))(inward[j].start)

    def finish(j):
        part = chunk(j, OUT_ROWS)

        @pl.when(is_hub)
        def _():
            swaps[j].wait_recv()
            for h in range(2):
                number = own[h, part] + crossed[h, part] + DAMPING * obj[h, part]
                out[h, part] = number * weight[part]
            pl.when(has_outer)(results[j].start)

    def chain(s):
        if s < steps:
            enter(s)
        if LAG_IN <= s < steps + LAG_IN:
            gather(s - LAG_IN)
        if s >= LAG_IN + LAG_CROSS:
            finish(s - LAG_IN - LAG_CROSS)

    def arrive(j):
        part = chunk(j, OUT_ROWS)

        @pl.when(has_above)
        def _():
            downs[j].wait_recv()
            for h in range(2):
                own[h, part] += upper[h, part]

    for k in range(PARTS):
        with scope(f"rb{k}"):
            rows_back(k)

    @pl.when(is_hub)
    def _():
        with scope("weight"):
            pl.when(has_above)(functools.partial(weigh, range(4)))
            weight[...] = 1.0 / weight[...]

    for s in range(steps + LAG_IN + LAG_CROSS):
        with scope(f"out{s}"):
            if s < steps:
                share_out(s)
                arrive(s)
            chain(s)

    @pl.when(jnp.logical_not(is_hub))
    def _():
        for j in range(steps):
            with scope(f"res{j}"):
                results[j].wait_recv()
                pl.when(has_outer)(results[j].start)

    def sent(there, src, send_sem):
        @pl.when(there)
        def _():
            send(src, src, s_send.at[send_sem], r_pass.at[0], east).wait_send()

    with scope("drain"):
        part = obj.at[:, :mid]
        sent(has_left, obj, 0)
        sent(has_above, part, 1)
        sent(has_below, part, 2)
        sent(has_below & has_left, part, 3)
        sent(has_below & has_left & odd_col, part, 4)
        sent(has_above & has_right & odd_col, part, 5)
        if layers > 1:
            sent(layers > 1, offs.at[0, pl.ds(0, layers - 1)], 6)
        sent(has_right, offs.at[0], 7)
        sent(has_below, offs.at[0], 8)
        sent(has_below & has_left, offs.at[0], 9)
        sent(has_right, terms, 10)
        sent(has_below, lower, 11)
        sent(jnp.logical_not(is_hub), own, 12)
        sent(is_hub, own, 13)
        sent(has_outer, out, 14)


def tables(side):
    mid = side // 2
    steps = np.arange(mid)
    kinds = []
    for shift in range(2):
        angle = (steps[:, None] * (2 * steps[None, :] + shift) % side) * (2.0 * np.pi / side)
        real, imag = np.cos(angle) / np.sqrt(side), -np.sin(angle) / np.sqrt(side)
        kinds.append(np.block([[real, imag], [-imag, real]]))
    both = np.stack(kinds)

    def halves(x):
        x = x.astype(np.float32)
        high = x.astype(jnp.bfloat16)
        return high, (x - high.astype(np.float32)).astype(jnp.bfloat16)

    return halves(both) + halves(both.transpose(0, 2, 1))


def body(sizes, object_field, probe_modes, amplitudes, offsets):
    rows, cols, layers = sizes
    side = object_field.shape[1]
    assert object_field.shape[2] == side and probe_modes.shape[2] == side
    assert offsets.shape[0] == 1 and layers % 2 == 0
    assert side % (PARTS * 2 * IN_ROWS) == 0 and side % (PARTS * OUT_ROWS) == 0
    modes = probe_modes.shape[1]
    hbm = pl.BlockSpec(memory_space=pltpu.MemorySpace.HBM)
    vmem = pl.BlockSpec(memory_space=pltpu.MemorySpace.VMEM)
    pair = (2, side, side)
    f32 = jnp.float32
    dma = pltpu.SemaphoreType.DMA
    tabs = tuple(jnp.asarray(t) for t in tables(side))
    tab = pltpu.VMEM((2, side, side), jnp.bfloat16)
    plane = pltpu.VMEM((side, side), f32)
    whole = pltpu.VMEM(pair, f32)
    corners = (4, layers, 1, 128)
    pieces, steps = side // IN_ROWS // 2, side // OUT_ROWS
    return pl.pallas_call(
        functools.partial(kernel, sizes),
        out_shape=pltpu.VMEM(pair, f32),
        in_specs=[hbm] * 8,
        out_specs=vmem,
        scratch_shapes=[
            pltpu.SMEM((1, 2), jnp.int32),
            whole,
            pltpu.VMEM(probe_modes.shape, f32),
            pltpu.VMEM((1, side, side), f32),
        ]
        + [tab] * 4
        + [pltpu.VMEM(corners, jnp.int32), pltpu.SMEM(corners, jnp.int32)]
        + [whole] * 3
        + [
            pltpu.VMEM(probe_modes.shape, f32),
            pltpu.VMEM((modes, 2, side, side), f32),
            pltpu.VMEM((modes, 2, side, side), f32),
        ]
        + [plane] * 3
        + [whole] * 7
        + [dma((8,)), dma(()), dma((15,)), dma((layers - 1,)), dma((3,))]
        + [dma((2 * pieces,))]
        + [dma((pieces,))] * 4
        + [dma((steps,))] * 4,
        compiler_params=pltpu.CompilerParams(
            collective_id=0, has_side_effects=True, vmem_limit_bytes=58 * 1024 * 1024
        ),
        name="update",
    )(offsets, object_field, probe_modes, amplitudes, *tabs)


def solution(mesh):
    sizes = tuple(mesh.shape[a] for a in AXES)
    placed = (
        P(None, "row", "col"),
        P(),
        P(("row", "col", "layer"), None, None),
        P(("row", "col", "layer"), None),
    )
    return jax.shard_map(
        functools.partial(body, sizes),
        mesh=mesh,
        in_specs=placed,
        out_specs=P(None, "row", "col"),
        check_vma=False,
    )
```

time: 54.5 us -> 46.5 us (0.85)
  Pallas kernels: 53.6 us -> 45.5 us
    pallas_call x1, Pallas kernels: 53.6 us -> 45.5 us  [body(): pl.pallas_call(functools.partial(kernel, sizes), out_shape=pltpu.VMEM(pai...]
where the time goes in v1:
time: 46.5 us; the launch traced here: 46.3 us
  Pallas kernels  45.5 us (98%)
  local copies, waits for them, and re-layouts  0.8 us (2%)
    pallas_call x1, Pallas kernels, body(): pl.pallas_call(functools.partial(kernel, sizes), out_shape=pltpu.VMEM(pai...  45.5 us

profile of v1, /device:TPU:6, one launch (start us, length us, event | category | flops | bytes accessed | tf_op | source)
XLA Modules:
  0.0 46.3 jit_solution(11573770978965264517)
XLA Ops:
  0.0 45.5 %update.1 = f32[2,256,256]{2,1,0:T(8,128)S(1)} custom-call(s32[1,2]{1,0:T(1,128)} %corner_hbm.1, f32[2,256,256]{2,1,0:T(8,128)} %obj_hbm.1, f32[2,4,256,256]{3,2,1,0:T(8,128)} %probe_hbm.1, f32[1,256,256]{2,1,0:T(8,128)} %amp_hbm.1, bf16[2,256,256]{2,1,0:T(8,128)(2,1)} %constant.8.clone.fwd_high_hbm, bf16[2,256,256]{2,1,0:T(8,128)(2,1)} %constant.9.clone.fwd_low_hbm, ...), custom_call_target="tpu_custom_call" | custom-call | tf_op jit(solution)/shard_map/update/pallas_call | solution.py:618
  45.6 0.8 %copy.10 = f32[2,256,256]{2,1,0:T(8,128)} copy(f32[2,256,256]{2,1,0:T(8,128)S(1)} %update.1) | data formatting | bytes 1048576

commit v2 on v1

--- a/solution.py
+++ b/solution.py
@@ -15,9 +15,11 @@
 PARTS = 4
 IN_ROWS = 16
 UNROLL = 4
+SIDE_ROWS = 16
 OUT_ROWS = 16
-LAG_IN = 3
-LAG_CROSS = 3
+LAG_IN = 8
+LAG_CROSS = 7
+GATE = 10
 
 
 def scope(name):
@@ -53,6 +55,8 @@
         (c < cols - 1, (r, c + 1, l)),
         (r > 0, (r - 1, c, l)),
         (r < rows - 1, (r + 1, c, l)),
+        ((r > 0) & (c < cols - 1), (r - 1, c + 1, l)),
+        ((r < rows - 1) & (c > 0), (r + 1, c - 1, l)),
     )
     for there, device in near:
         pl.when(there)(functools.partial(tell, device))
@@ -91,7 +95,7 @@
     right, below, diag, rolled, lines, far, ratio, power, weight,
     terms, left, own, lower, upper, inbound, crossed,
     s_load, s_corner, s_send, r_off, r_pass,
-    r_right, r_below, r_share, r_diag, r_diag2, r_left, r_down, r_in, r_last,
+    r_right, r_right2, r_below, r_share, r_diag, r_diag2, r_left, r_down, r_in, r_last, gate,
 ):
     rows, cols, layers = sizes
     side = obj.shape[1]
@@ -146,13 +150,17 @@
     lefts, lefts2, ups, shares, diags, diags2, extras = [], [], [], [], [], [], []
     for i in range(pieces):
         mine, other = chunk(2 * i + odd, IN_ROWS), chunk(2 * i + 1 - odd, IN_ROWS)
-        lefts.append(piece(obj, right, mine, 0, r_right.at[i], west))
-        lefts2.append(piece(obj, right, other, 0, r_right.at[pieces + i], west))
+        lefts.append(piece(obj, right, mine, 0, r_right.at[i // 2], west))
+        lefts2.append(piece(obj, right, other, 0, r_right2.at[i // 2], west))
         ups.append(piece(obj, below, mine, 1, r_below.at[i], north))
         shares.append(piece(below, below, mine, 2, r_share.at[i], partner))
-        diags.append(piece(below, diag, mine, 3, r_diag.at[i], west))
-        diags2.append(piece(below, diag, other, 4, r_diag2.at[i], west))
-        extras.append(piece(right, diag, other, 5, r_diag2.at[i], north))
+        diags.append(piece(below, diag, mine, 3, r_diag.at[i // 2], west))
+        diags2.append(piece(below, diag, other, 4, r_diag2.at[i // 2], west))
+        extras.append(piece(right, diag, other, 5, r_diag2.at[i // 2], north))
+
+    def two(recv_sem):
+        piece(obj, right, chunk(0, 2 * IN_ROWS), 0, recv_sem, west).wait_recv()
+
     for copy in ups:
         pl.when(has_above)(copy.start)
     for copy in lefts2 + lefts:
@@ -182,10 +190,13 @@
             shares[i].start()
             pl.when(has_left)(diags[i].start)
 
-        @pl.when(has_above & has_right & odd_col)
-        def _():
-            lefts2[i].wait_recv()
-            extras[i].start()
+        if i % 2 == 0:
+
+            @pl.when(has_above & has_right & odd_col)
+            def _():
+                two(r_right2.at[i // 2])
+                extras[i].start()
+                extras[i + 1].start()
 
     def forward2(i):
         @pl.when(has_below)
@@ -286,28 +297,6 @@
             offs[3] = jnp.zeros(offs.shape[1:], jnp.int32)
             fetched.start()
 
-    quarters = [(g, q * layers // 2, (q + 1) * layers // 2) for g in (0, 1) for q in range(2)]
-    for i in range(3, pieces + 4):
-        with scope(f"fwd{i}"):
-            if i < pieces:
-                forward(i)
-            if i >= 4:
-                forward2(i - 4)
-        if 3 < i < 8:
-
-            @pl.when(jnp.logical_not(has_above) & is_hub)
-            def _(i=i):
-                with scope(f"weight{i}"):
-                    if i == 4:
-                        fetched.wait()
-                    group, start, stop = quarters[i - 4]
-                    weigh((group,), start, stop)
-
-    pl.when(jnp.logical_not(has_above | is_hub))(fetched.wait)
-
-    with scope("loads"):
-        for copy in loads[4:]:
-            copy.wait()
     fwd, inv = (fwd_high, fwd_low), (inv_high, inv_low)
 
     def after(x, table, which):
@@ -318,9 +307,8 @@
 
     lane = lax.broadcasted_iota(jnp.int32, (tall, side), 1)
     line = lax.broadcasted_iota(jnp.int32, (tall, side), 0)
-    per_part_in = tall // IN_ROWS // 2
-
-    for k in range(PARTS):
+
+    def first_part(k):
         part = chunk(k, tall)
         with scope(f"merge{k}"):
             high = line + k * tall < down
@@ -329,13 +317,11 @@
 
             @pl.when(has_right & jnp.logical_not(has_above & odd_col))
             def _():
-                for i in range(k * per_part_in, (k + 1) * per_part_in):
-                    lefts2[i].wait_recv()
+                two(r_right2.at[k])
 
             @pl.when(has_right)
             def _():
-                for i in range(k * per_part_in, (k + 1) * per_part_in):
-                    lefts[i].wait_recv()
+                two(r_right.at[k])
                 for h in range(2):
                     own[h, part] = jnp.where(lane < over, right[h, part], own[h, part])
 
@@ -346,9 +332,8 @@
 
             @pl.when(has_below & has_right)
             def _():
-                for i in range(k * per_part_in, (k + 1) * per_part_in):
-                    diags[i].wait_recv()
-                    diags2[i].wait_recv()
+                two(r_diag.at[k])
+                two(r_diag2.at[k])
                 for h in range(2):
                     own[h, part] = jnp.where(high & (lane < over), diag[h, part], own[h, part])
 
@@ -370,6 +355,37 @@
                         [even[here, there], uneven[here, there]], axis=1
                     )
 
+    early = has_below & jnp.logical_not(odd_col & has_right)
+    quarters = [(g, q * layers // 2, (q + 1) * layers // 2) for g in (0, 1) for q in range(2)]
+    with scope("loads"):
+        for copy in loads[4:]:
+            copy.wait()
+    for i in range(3, pieces):
+        with scope(f"fwd{i}"):
+            forward(i)
+    for i in range(pieces):
+        with scope(f"fwz{i}"):
+            forward2(i)
+        if i < 4:
+
+            @pl.when(jnp.logical_not(has_above) & is_hub)
+            def _(i=i):
+                with scope(f"weight{i}"):
+                    if i == 0:
+                        fetched.wait()
+                    group, start, stop = quarters[i]
+                    weigh((group,), start, stop)
+
+        if i % 2 == 1 and i > 1:
+            pl.when(early)(functools.partial(first_part, i // 2 - 1))
+    pl.when(early)(functools.partial(first_part, PARTS - 1))
+    pl.when(jnp.logical_not(has_above | is_hub))(fetched.wait)
+
+    @pl.when(jnp.logical_not(early))
+    def _():
+        for k in range(PARTS):
+            first_part(k)
+
     ratio[...] = jnp.zeros_like(ratio)
 
     def columns(m, carry):
@@ -418,18 +434,19 @@
 
     left_down, left_over = corner_of(corners, 1, l, side)
 
-    def flow(src, dst, send_sem, recv_sem, device):
+    def flow(src, dst, send_sem, recv_sem, device, size=OUT_ROWS):
         return [
-            piece(src, dst, chunk(k, OUT_ROWS), send_sem, recv_sem.at[k], device)
-            for k in range(steps)
+            piece(src, dst, chunk(k, size), send_sem, recv_sem.at[k], device)
+            for k in range(side // size)
         ]
 
-    rights = flow(terms, left, 10, r_left, east)
+    rights = flow(terms, left, 10, r_left, east, SIDE_ROWS)
     downs = flow(lower, upper, 11, r_down, south)
     inward = flow(own, inbound, 12, r_in, inner)
     swaps = flow(own, crossed, 13, r_last, inner)
     results = flow(out, out, 14, r_last, outer)
-    per_tall = tall // OUT_ROWS
+    per_tall = tall // SIDE_ROWS
+    per_side = SIDE_ROWS // OUT_ROWS
 
     def rows_back(k):
         part = chunk(k, tall)
@@ -475,7 +492,8 @@
 
         @pl.when(has_left)
         def _():
-            rights[j].wait_recv()
+            if j % per_side == 0:
+                rights[j // per_side].wait_recv()
             for h in range(2):
                 other = jnp.where(thin_lane < left_over, left[h, part], 0.0)
                 own[h, part] += jnp.where(at >= left_down, other, 0.0)
@@ -529,6 +547,13 @@
             downs[j].wait_recv()
             for h in range(2):
                 own[h, part] += upper[h, part]
+            if j == GATE:
+
+                @pl.when(jnp.logical_not(odd_col) & has_right)
+                def _():
+                    pl.semaphore_signal(
+                        gate, 1, device_id=(r - 1, c + 1, l), device_id_type=pl.DeviceIdType.MESH
+                    )
 
     for k in range(PARTS):
         with scope(f"rb{k}"):
@@ -539,6 +564,11 @@
         with scope("weight"):
             pl.when(has_above)(functools.partial(weigh, range(4)))
             weight[...] = 1.0 / weight[...]
+
+    @pl.when(has_below & odd_col)
+    def _():
+        with scope("gate"):
+            pl.semaphore_wait(gate, 1)
 
     for s in range(steps + LAG_IN + LAG_CROSS):
         with scope(f"out{s}"):
@@ -602,7 +632,8 @@
     side = object_field.shape[1]
     assert object_field.shape[2] == side and probe_modes.shape[2] == side
     assert offsets.shape[0] == 1 and layers % 2 == 0
-    assert side % (PARTS * 2 * IN_ROWS) == 0 and side % (PARTS * OUT_ROWS) == 0
+    assert side == PARTS * 4 * IN_ROWS
+    assert side % (PARTS * SIDE_ROWS) == 0 and SIDE_ROWS % OUT_ROWS == 0
     modes = probe_modes.shape[1]
     hbm = pl.BlockSpec(memory_space=pltpu.MemorySpace.HBM)
     vmem = pl.BlockSpec(memory_space=pltpu.MemorySpace.VMEM)
@@ -637,9 +668,12 @@
         + [plane] * 3
         + [whole] * 7
         + [dma((8,)), dma(()), dma((15,)), dma((layers - 1,)), dma((3,))]
-        + [dma((2 * pieces,))]
-        + [dma((pieces,))] * 4
-        + [dma((steps,))] * 4,
+        + [dma((pieces // 2,))] * 2
+        + [dma((pieces,))] * 2
+        + [dma((pieces // 2,))] * 2
+        + [dma((side // SIDE_ROWS,))]
+        + [dma((steps,))] * 3
+        + [pltpu.SemaphoreType.REGULAR],
         compiler_params=pltpu.CompilerParams(
             collective_id=0, has_side_effects=True, vmem_limit_bytes=58 * 1024 * 1024
         ),

time: 46.5 us -> 44.3 us (0.953)
  the two profiles are of different devices: /device:TPU:6 before, /device:TPU:3 now
where the time goes in v2:
time: 44.3 us; the launch traced here: 44.2 us
  Pallas kernels  43.4 us (98%)
  local copies, waits for them, and re-layouts  0.8 us (2%)
    pallas_call x1, Pallas kernels, body(): pl.pallas_call(functools.partial(kernel, sizes), out_shape=pltpu.VMEM(pai...  43.4 us

profile of v2, /device:TPU:3, one launch (start us, length us, event | category | flops | bytes accessed | tf_op | source)
XLA Modules:
  0.0 44.2 jit_solution(9587863194799085579)
XLA Ops:
  0.0 43.4 %update.1 = f32[2,256,256]{2,1,0:T(8,128)S(1)} custom-call(s32[1,2]{1,0:T(1,128)} %corner_hbm.1, f32[2,256,256]{2,1,0:T(8,128)} %obj_hbm.1, f32[2,4,256,256]{3,2,1,0:T(8,128)} %probe_hbm.1, f32[1,256,256]{2,1,0:T(8,128)} %amp_hbm.1, bf16[2,256,256]{2,1,0:T(8,128)(2,1)} %constant.8.clone.fwd_high_hbm, bf16[2,256,256]{2,1,0:T(8,128)(2,1)} %constant.9.clone.fwd_low_hbm, ...), custom_call_target="tpu_custom_call" | custom-call | tf_op jit(solution)/shard_map/update/pallas_call | solution.py:649
  43.4 0.8 %copy.10 = f32[2,256,256]{2,1,0:T(8,128)} copy(f32[2,256,256]{2,1,0:T(8,128)S(1)} %update.1) | data formatting | bytes 1048576

commit v3 on v2

--- a/solution.py
+++ b/solution.py
@@ -15,11 +15,12 @@
 PARTS = 4
 IN_ROWS = 16
 UNROLL = 4
-SIDE_ROWS = 16
 OUT_ROWS = 16
 LAG_IN = 8
 LAG_CROSS = 7
-GATE = 10
+GATE = 7
+HEAD = 4
+OVER_SIDE = 6
 
 
 def scope(name):
@@ -89,13 +90,13 @@
 
 def kernel(
     sizes,
-    corner_hbm, obj_hbm, probe_hbm, amp_hbm, fwd_high_hbm, fwd_low_hbm, inv_high_hbm, inv_low_hbm,
+    corner_hbm, obj_hbm, probe_hbm, amp_hbm, table_hbm,
     out,
-    corner, obj, probe, amp, fwd_high, fwd_low, inv_high, inv_low, offs, corners,
-    right, below, diag, rolled, lines, far, ratio, power, weight,
+    corner, obj, probe, amp, table, offs, corners,
+    right, below, diag, rolled, lines, far, parted, ratio, power, weight,
     terms, left, own, lower, upper, inbound, crossed,
     s_load, s_corner, s_send, r_off, r_pass,
-    r_right, r_right2, r_below, r_share, r_diag, r_diag2, r_left, r_down, r_in, r_last, gate,
+    r_right, r_right2, r_pool, r_left, r_in, r_last, gate,
 ):
     rows, cols, layers = sizes
     side = obj.shape[1]
@@ -127,10 +128,7 @@
                 (obj_hbm, obj),
                 (probe_hbm, probe),
                 (amp_hbm, amp),
-                (fwd_high_hbm, fwd_high),
-                (fwd_low_hbm, fwd_low),
-                (inv_high_hbm, inv_high),
-                (inv_low_hbm, inv_low),
+                (table_hbm, table),
             )
         )
     ]
@@ -147,23 +145,25 @@
     def piece(src, dst, part, send_sem, recv_sem, device):
         return send(src.at[:, part], dst.at[:, part], s_send.at[send_sem], recv_sem, device)
 
-    lefts, lefts2, ups, shares, diags, diags2, extras = [], [], [], [], [], [], []
+    lefts, lefts2, ups, shares, diags, diags2, extras, extras2 = ([] for _ in range(8))
     for i in range(pieces):
         mine, other = chunk(2 * i + odd, IN_ROWS), chunk(2 * i + 1 - odd, IN_ROWS)
         lefts.append(piece(obj, right, mine, 0, r_right.at[i // 2], west))
         lefts2.append(piece(obj, right, other, 0, r_right2.at[i // 2], west))
-        ups.append(piece(obj, below, mine, 1, r_below.at[i], north))
-        shares.append(piece(below, below, mine, 2, r_share.at[i], partner))
-        diags.append(piece(below, diag, mine, 3, r_diag.at[i // 2], west))
-        diags2.append(piece(below, diag, other, 4, r_diag2.at[i // 2], west))
-        extras.append(piece(right, diag, other, 5, r_diag2.at[i // 2], north))
+        ups.append(piece(obj, below, mine, 1, r_pool.at[i], north))
+        shares.append(piece(below, below, mine, 2, r_pool.at[pieces + i], partner))
+        diags.append(piece(below, diag, mine, 3, r_pool.at[2 * pieces + i // 2], west))
+        diags2.append(piece(below, diag, other, 4, r_pool.at[2 * pieces + (pieces + i) // 2], west))
+        if i >= OVER_SIDE:
+            extras2.append(piece(right, diag, mine, 5, r_pool.at[2 * pieces + i // 2], north))
+        extras.append(piece(right, diag, other, 5, r_pool.at[2 * pieces + (pieces + i) // 2], north))
 
     def two(recv_sem):
         piece(obj, right, chunk(0, 2 * IN_ROWS), 0, recv_sem, west).wait_recv()
 
     for copy in ups:
         pl.when(has_above)(copy.start)
-    for copy in lefts2 + lefts:
+    for copy in lefts2 + lefts[OVER_SIDE:] + lefts[:OVER_SIDE]:
         pl.when(has_left)(copy.start)
     with scope("load0"):
         loads[0].wait()
@@ -188,7 +188,7 @@
         def _():
             ups[i].wait_recv()
             shares[i].start()
-            pl.when(has_left)(diags[i].start)
+            pl.when(has_left & odd_col if i >= OVER_SIDE else has_left)(diags[i].start)
 
         if i % 2 == 0:
 
@@ -197,6 +197,11 @@
                 two(r_right2.at[i // 2])
                 extras[i].start()
                 extras[i + 1].start()
+                if i + 2 == pieces:
+                    for k in range(OVER_SIDE // 2, pieces // 2):
+                        two(r_right.at[k])
+                    for copy in extras2:
+                        copy.start()
 
     def forward2(i):
         @pl.when(has_below)
@@ -297,7 +302,7 @@
             offs[3] = jnp.zeros(offs.shape[1:], jnp.int32)
             fetched.start()
 
-    fwd, inv = (fwd_high, fwd_low), (inv_high, inv_low)
+    fwd, inv = (table.at[0], table.at[1]), (table.at[2], table.at[3])
 
     def after(x, table, which):
         return prod(split(x), (table[0][which], table[1][which]))
@@ -319,9 +324,11 @@
             def _():
                 two(r_right2.at[k])
 
+            ready = has_above & odd_col if k >= OVER_SIDE // 2 else has_right & False
+            pl.when(has_right & jnp.logical_not(ready))(lambda: two(r_right.at[k]))
+
             @pl.when(has_right)
             def _():
-                two(r_right.at[k])
                 for h in range(2):
                     own[h, part] = jnp.where(lane < over, right[h, part], own[h, part])
 
@@ -332,8 +339,8 @@
 
             @pl.when(has_below & has_right)
             def _():
-                two(r_diag.at[k])
-                two(r_diag2.at[k])
+                two(r_pool.at[2 * pieces + k])
+                two(r_pool.at[2 * pieces + pieces // 2 + k])
                 for h in range(2):
                     own[h, part] = jnp.where(high & (lane < over), diag[h, part], own[h, part])
 
@@ -403,21 +410,30 @@
         lax.fori_loop(0, modes, columns, 0, unroll=UNROLL)
     ratio[...] = amp[0] / (jnp.sqrt(ratio[...]) + SOFTEN)
 
-    def back(m, carry):
-        turned = []
-        for which in range(2):
-            scale = ratio[which * mid : (which + 1) * mid]
-            fixed = jnp.concatenate([far[m, which, :mid] * scale, far[m, which, mid:] * scale], axis=0)
-            turned.append(ahead(fwd, which, fixed))
-        total, gap = turned[0] + turned[1], turned[0] - turned[1]
-        for h in range(2):
-            there = slice(h * mid, (h + 1) * mid)
-            lines[m, h, :mid] = total[there]
-            lines[m, h, mid:] = gap[there]
-        return carry
-
-    with scope("back"):
-        lax.fori_loop(0, modes, back, 0, unroll=UNROLL)
+    def back(p):
+        near = (slice(p * tall, (p + 1) * tall), slice(mid + p * tall, mid + (p + 1) * tall))
+        for m in range(modes):
+            turned = []
+            for which in range(2):
+                if p == 0:
+                    scale = ratio[which * mid : (which + 1) * mid]
+                    fixed = jnp.concatenate(
+                        [far[m, which, :mid] * scale, far[m, which, mid:] * scale], axis=0
+                    )
+                    halves = split(fixed)
+                    for x in range(2):
+                        parted[x, m, which] = halves[x]
+                else:
+                    halves = (parted[0, m, which], parted[1, m, which])
+                rows_of = [
+                    jnp.concatenate([t[which, here] for here in near], axis=0) for t in fwd
+                ]
+                turned.append(prod(rows_of, halves))
+            total, gap = turned[0] + turned[1], turned[0] - turned[1]
+            for h in range(2):
+                there = slice(h * tall, (h + 1) * tall)
+                lines[m, h, near[0]] = total[there]
+                lines[m, h, near[1]] = gap[there]
 
     @pl.when(has_above)
     def _():
@@ -434,19 +450,20 @@
 
     left_down, left_over = corner_of(corners, 1, l, side)
 
-    def flow(src, dst, send_sem, recv_sem, device, size=OUT_ROWS):
+    per_tall = tall // OUT_ROWS
+    order = [k * per_tall + i for p in range(2) for k in (p, p + 2) for i in range(per_tall)]
+
+    def flow(src, dst, send_sem, recv_sem, device, base=0):
         return [
-            piece(src, dst, chunk(k, size), send_sem, recv_sem.at[k], device)
-            for k in range(side // size)
+            piece(src, dst, chunk(order[k], OUT_ROWS), send_sem, recv_sem.at[base + k], device)
+            for k in range(steps)
         ]
 
-    rights = flow(terms, left, 10, r_left, east, SIDE_ROWS)
-    downs = flow(lower, upper, 11, r_down, south)
+    rights = flow(terms, left, 10, r_left, east)
+    downs = flow(lower, upper, 11, r_pool, south, base=3 * pieces if rows > 2 else 0)
     inward = flow(own, inbound, 12, r_in, inner)
     swaps = flow(own, crossed, 13, r_last, inner)
     results = flow(out, out, 14, r_last, outer)
-    per_tall = tall // SIDE_ROWS
-    per_side = SIDE_ROWS // OUT_ROWS
 
     def rows_back(k):
         part = chunk(k, tall)
@@ -476,15 +493,16 @@
 
         @pl.when(has_right)
         def _():
-            for j in range(k * per_tall, (k + 1) * per_tall):
-                rights[j].start()
+            for j in range(steps):
+                if order[j] // per_tall == k:
+                    rights[j].start()
 
     thin_lane = lax.broadcasted_iota(jnp.int32, (OUT_ROWS, side), 1)
     thin_line = lax.broadcasted_iota(jnp.int32, (OUT_ROWS, side), 0)
 
     def share_out(j):
-        part = chunk(j, OUT_ROWS)
-        at = thin_line + j * OUT_ROWS
+        part = chunk(order[j], OUT_ROWS)
+        at = thin_line + order[j] * OUT_ROWS
         for h in range(2):
             mine = jnp.where(thin_lane >= over, terms[h, part], 0.0)
             own[h, part] = jnp.where(at >= down, mine, 0.0)
@@ -492,8 +510,7 @@
 
         @pl.when(has_left)
         def _():
-            if j % per_side == 0:
-                rights[j // per_side].wait_recv()
+            rights[j].wait_recv()
             for h in range(2):
                 other = jnp.where(thin_lane < left_over, left[h, part], 0.0)
                 own[h, part] += jnp.where(at >= left_down, other, 0.0)
@@ -510,7 +527,7 @@
                 inward[j].start()
 
     def gather(j):
-        part = chunk(j, OUT_ROWS)
+        part = chunk(order[j], OUT_ROWS)
 
         @pl.when(has_outer)
         def _():
@@ -521,7 +538,7 @@
             pl.when(jnp.logical_not(is_hub))(inward[j].start)
 
     def finish(j):
-        part = chunk(j, OUT_ROWS)
+        part = chunk(order[j], OUT_ROWS)
 
         @pl.when(is_hub)
         def _():
@@ -531,16 +548,8 @@
                 out[h, part] = number * weight[part]
             pl.when(has_outer)(results[j].start)
 
-    def chain(s):
-        if s < steps:
-            enter(s)
-        if LAG_IN <= s < steps + LAG_IN:
-            gather(s - LAG_IN)
-        if s >= LAG_IN + LAG_CROSS:
-            finish(s - LAG_IN - LAG_CROSS)
-
     def arrive(j):
-        part = chunk(j, OUT_ROWS)
+        part = chunk(order[j], OUT_ROWS)
 
         @pl.when(has_above)
         def _():
@@ -555,9 +564,23 @@
                         gate, 1, device_id=(r - 1, c + 1, l), device_id_type=pl.DeviceIdType.MESH
                     )
 
-    for k in range(PARTS):
-        with scope(f"rb{k}"):
-            rows_back(k)
+    begun = jnp.logical_not(has_above) & (odd_col | jnp.logical_not(has_left))
+
+    def begin(stop):
+        for s in range(stop):
+            share_out(s)
+            enter(s)
+
+    for p in range(2):
+        with scope(f"back{p}"):
+            back(p)
+        for k in (p, p + 2):
+            with scope(f"rb{k}"):
+                rows_back(k)
+        if p == 0:
+            with scope("begin"):
+                pl.when(begun & odd_col)(functools.partial(begin, HEAD))
+                pl.when(begun & jnp.logical_not(odd_col))(functools.partial(begin, steps // 2))
 
     @pl.when(is_hub)
     def _():
@@ -565,17 +588,39 @@
             pl.when(has_above)(functools.partial(weigh, range(4)))
             weight[...] = 1.0 / weight[...]
 
-    @pl.when(has_below & odd_col)
+    def run(first, stop):
+        for s in range(first, stop + LAG_IN + LAG_CROSS):
+            with scope(f"out{s}"):
+                if s < stop:
+                    if s < (steps // 2 if first == 0 and stop == steps else HEAD):
+
+                        @pl.when(jnp.logical_not(begun))
+                        def _(s=s):
+                            share_out(s)
+                            arrive(s)
+                            enter(s)
+
+                    else:
+                        share_out(s)
+                        arrive(s)
+                        enter(s)
+                if first <= s - LAG_IN < stop:
+                    gather(s - LAG_IN)
+                if first <= s - LAG_IN - LAG_CROSS:
+                    finish(s - LAG_IN - LAG_CROSS)
+
+    pl.when(jnp.logical_not(odd_col))(functools.partial(run, 0, steps))
+
+    @pl.when(odd_col)
     def _():
-        with scope("gate"):
-            pl.semaphore_wait(gate, 1)
-
-    for s in range(steps + LAG_IN + LAG_CROSS):
-        with scope(f"out{s}"):
-            if s < steps:
-                share_out(s)
-                arrive(s)
-            chain(s)
+        run(0, HEAD)
+
+        @pl.when(has_below)
+        def _():
+            with scope("gate"):
+                pl.semaphore_wait(gate, 1)
+
+        run(HEAD, steps)
 
     @pl.when(jnp.logical_not(is_hub))
     def _():
@@ -594,9 +639,12 @@
         sent(has_left, obj, 0)
         sent(has_above, part, 1)
         sent(has_below, part, 2)
-        sent(has_below & has_left, part, 3)
+        sent(has_below & has_left & odd_col, part, 3)
+        few = obj.at[:, : OVER_SIDE * IN_ROWS]
+        sent(has_below & has_left & jnp.logical_not(odd_col), few, 3)
         sent(has_below & has_left & odd_col, part, 4)
-        sent(has_above & has_right & odd_col, part, 5)
+        many = obj.at[:, : (2 * pieces - OVER_SIDE) * IN_ROWS]
+        sent(has_above & has_right & odd_col, many, 5)
         if layers > 1:
             sent(layers > 1, offs.at[0, pl.ds(0, layers - 1)], 6)
         sent(has_right, offs.at[0], 7)
@@ -624,7 +672,7 @@
         high = x.astype(jnp.bfloat16)
         return high, (x - high.astype(np.float32)).astype(jnp.bfloat16)
 
-    return halves(both) + halves(both.transpose(0, 2, 1))
+    return np.stack(halves(both) + halves(both.transpose(0, 2, 1)))
 
 
 def body(sizes, object_field, probe_modes, amplitudes, offsets):
@@ -632,16 +680,14 @@
     side = object_field.shape[1]
     assert object_field.shape[2] == side and probe_modes.shape[2] == side
     assert offsets.shape[0] == 1 and layers % 2 == 0
-    assert side == PARTS * 4 * IN_ROWS
-    assert side % (PARTS * SIDE_ROWS) == 0 and SIDE_ROWS % OUT_ROWS == 0
+    assert side == PARTS * 4 * IN_ROWS and side // OUT_ROWS <= 3 * (side // IN_ROWS // 2)
+    assert PARTS == 4 and side % (PARTS * OUT_ROWS) == 0
     modes = probe_modes.shape[1]
     hbm = pl.BlockSpec(memory_space=pltpu.MemorySpace.HBM)
     vmem = pl.BlockSpec(memory_space=pltpu.MemorySpace.VMEM)
     pair = (2, side, side)
     f32 = jnp.float32
     dma = pltpu.SemaphoreType.DMA
-    tabs = tuple(jnp.asarray(t) for t in tables(side))
-    tab = pltpu.VMEM((2, side, side), jnp.bfloat16)
     plane = pltpu.VMEM((side, side), f32)
     whole = pltpu.VMEM(pair, f32)
     corners = (4, layers, 1, 128)
@@ -649,7 +695,7 @@
     return pl.pallas_call(
         functools.partial(kernel, sizes),
         out_shape=pltpu.VMEM(pair, f32),
-        in_specs=[hbm] * 8,
+        in_specs=[hbm] * 5,
         out_specs=vmem,
         scratch_shapes=[
             pltpu.SMEM((1, 2), jnp.int32),
@@ -657,28 +703,27 @@
             pltpu.VMEM(probe_modes.shape, f32),
             pltpu.VMEM((1, side, side), f32),
         ]
-        + [tab] * 4
+        + [pltpu.VMEM((4, 2, side, side), jnp.bfloat16)]
         + [pltpu.VMEM(corners, jnp.int32), pltpu.SMEM(corners, jnp.int32)]
         + [whole] * 3
         + [
             pltpu.VMEM(probe_modes.shape, f32),
             pltpu.VMEM((modes, 2, side, side), f32),
             pltpu.VMEM((modes, 2, side, side), f32),
+            pltpu.VMEM((2, modes, 2, side, side), jnp.bfloat16),
         ]
         + [plane] * 3
         + [whole] * 7
-        + [dma((8,)), dma(()), dma((15,)), dma((layers - 1,)), dma((3,))]
+        + [dma((5,)), dma(()), dma((15,)), dma((layers - 1,)), dma((3,))]
         + [dma((pieces // 2,))] * 2
-        + [dma((pieces,))] * 2
-        + [dma((pieces // 2,))] * 2
-        + [dma((side // SIDE_ROWS,))]
+        + [dma((3 * pieces + (steps if rows > 2 else 0),))]
         + [dma((steps,))] * 3
         + [pltpu.SemaphoreType.REGULAR],
         compiler_params=pltpu.CompilerParams(
             collective_id=0, has_side_effects=True, vmem_limit_bytes=58 * 1024 * 1024
         ),
         name="update",
-    )(offsets, object_field, probe_modes, amplitudes, *tabs)
+    )(offsets, object_field, probe_modes, amplitudes, jnp.asarray(tables(side)))
 
 
 def solution(mesh):

time: 44.3 us -> 42.9 us (0.968)
  Pallas kernels: 43.4 us -> 41.9 us
    pallas_call x1, Pallas kernels: 43.4 us -> 41.9 us  [body(): pl.pallas_call(functools.partial(kernel, sizes), out_shape=pltpu.VMEM(pai...]
where the time goes in v3:
time: 42.9 us; the launch traced here: 42.7 us
  Pallas kernels  41.9 us (98%)
  local copies, waits for them, and re-layouts  0.8 us (2%)
    pallas_call x1, Pallas kernels, body(): pl.pallas_call(functools.partial(kernel, sizes), out_shape=pltpu.VMEM(pai...  41.9 us

profile of v3, /device:TPU:3, one launch (start us, length us, event | category | flops | bytes accessed | tf_op | source)
XLA Modules:
  0.0 42.7 jit_solution(8285823290279360118)
XLA Ops:
  0.0 41.9 %update.1 = f32[2,256,256]{2,1,0:T(8,128)S(1)} custom-call(s32[1,2]{1,0:T(1,128)} %corner_hbm.1, f32[2,256,256]{2,1,0:T(8,128)} %obj_hbm.1, f32[2,4,256,256]{3,2,1,0:T(8,128)} %probe_hbm.1, f32[1,256,256]{2,1,0:T(8,128)} %amp_hbm.1, bf16[4,2,256,256]{3,2,1,0:T(8,128)(2,1)} %constant.2.clone.table_hbm), custom_call_target="tpu_custom_call" | custom-call | tf_op jit(solution)/shard_map/update/pallas_call | solution.py:695
  41.9 0.8 %copy.7 = f32[2,256,256]{2,1,0:T(8,128)} copy(f32[2,256,256]{2,1,0:T(8,128)S(1)} %update.1) | data formatting | bytes 1048576

commit v4 on v3

--- a/solution.py
+++ b/solution.py
@@ -16,9 +16,9 @@
 IN_ROWS = 16
 UNROLL = 4
 OUT_ROWS = 16
-LAG_IN = 8
+LAG_IN = 6
 LAG_CROSS = 7
-GATE = 7
+GATE = 10
 HEAD = 4
 OVER_SIDE = 6
 

time: 42.9 us -> 42.5 us (level)
  no operation moved by 1% of the time
where the time goes in v4:
time: 42.5 us; the launch traced here: 42.4 us
  Pallas kernels  41.6 us (98%)
  local copies, waits for them, and re-layouts  0.8 us (2%)
    pallas_call x1, Pallas kernels, body(): pl.pallas_call(functools.partial(kernel, sizes), out_shape=pltpu.VMEM(pai...  41.6 us

profile of v4, /device:TPU:3, one launch (start us, length us, event | category | flops | bytes accessed | tf_op | source)
XLA Modules:
  0.0 42.4 jit_solution(3422843668178977527)
XLA Ops:
  0.0 41.6 %update.1 = f32[2,256,256]{2,1,0:T(8,128)S(1)} custom-call(s32[1,2]{1,0:T(1,128)} %corner_hbm.1, f32[2,256,256]{2,1,0:T(8,128)} %obj_hbm.1, f32[2,4,256,256]{3,2,1,0:T(8,128)} %probe_hbm.1, f32[1,256,256]{2,1,0:T(8,128)} %amp_hbm.1, bf16[4,2,256,256]{3,2,1,0:T(8,128)(2,1)} %constant.2.clone.table_hbm), custom_call_target="tpu_custom_call" | custom-call | tf_op jit(solution)/shard_map/update/pallas_call | solution.py:695
  41.6 0.8 %copy.7 = f32[2,256,256]{2,1,0:T(8,128)} copy(f32[2,256,256]{2,1,0:T(8,128)S(1)} %update.1) | data formatting | bytes 1048576

commit v5 on v4

--- a/solution.py
+++ b/solution.py
@@ -16,8 +16,8 @@
 IN_ROWS = 16
 UNROLL = 4
 OUT_ROWS = 16
-LAG_IN = 6
-LAG_CROSS = 7
+EVEN_LAGS = (6, 8)
+ODD_LAGS = (5, 7)
 GATE = 10
 HEAD = 4
 OVER_SIDE = 6
@@ -588,8 +588,9 @@
             pl.when(has_above)(functools.partial(weigh, range(4)))
             weight[...] = 1.0 / weight[...]
 
-    def run(first, stop):
-        for s in range(first, stop + LAG_IN + LAG_CROSS):
+    def run(first, stop, lags):
+        lag_in, lag_cross = lags
+        for s in range(first, stop + lag_in + lag_cross):
             with scope(f"out{s}"):
                 if s < stop:
                     if s < (steps // 2 if first == 0 and stop == steps else HEAD):
@@ -604,23 +605,23 @@
                         share_out(s)
                         arrive(s)
                         enter(s)
-                if first <= s - LAG_IN < stop:
-                    gather(s - LAG_IN)
-                if first <= s - LAG_IN - LAG_CROSS:
-                    finish(s - LAG_IN - LAG_CROSS)
-
-    pl.when(jnp.logical_not(odd_col))(functools.partial(run, 0, steps))
+                if first <= s - lag_in < stop:
+                    gather(s - lag_in)
+                if first <= s - lag_in - lag_cross:
+                    finish(s - lag_in - lag_cross)
+
+    pl.when(jnp.logical_not(odd_col))(functools.partial(run, 0, steps, EVEN_LAGS))
 
     @pl.when(odd_col)
     def _():
-        run(0, HEAD)
+        run(0, HEAD, ODD_LAGS)
 
         @pl.when(has_below)
         def _():
             with scope("gate"):
                 pl.semaphore_wait(gate, 1)
 
-        run(HEAD, steps)
+        run(HEAD, steps, ODD_LAGS)
 
     @pl.when(jnp.logical_not(is_hub))
     def _():

time: 42.5 us -> 42.2 us (level)
  no operation moved by 1% of the time
where the time goes in v5:
time: 42.2 us; the launch traced here: 42.1 us
  Pallas kernels  41.3 us (98%)
  local copies, waits for them, and re-layouts  0.8 us (2%)
    pallas_call x1, Pallas kernels, body(): pl.pallas_call(functools.partial(kernel, sizes), out_shape=pltpu.VMEM(pai...  41.3 us

profile of v5, /device:TPU:3, one launch (start us, length us, event | category | flops | bytes accessed | tf_op | source)
XLA Modules:
  0.0 42.1 jit_solution(3489412513648375602)
XLA Ops:
  0.0 41.3 %update.1 = f32[2,256,256]{2,1,0:T(8,128)S(1)} custom-call(s32[1,2]{1,0:T(1,128)} %corner_hbm.1, f32[2,256,256]{2,1,0:T(8,128)} %obj_hbm.1, f32[2,4,256,256]{3,2,1,0:T(8,128)} %probe_hbm.1, f32[1,256,256]{2,1,0:T(8,128)} %amp_hbm.1, bf16[4,2,256,256]{3,2,1,0:T(8,128)(2,1)} %constant.2.clone.table_hbm), custom_call_target="tpu_custom_call" | custom-call | tf_op jit(solution)/shard_map/update/pallas_call | solution.py:696
  41.3 0.8 %copy.7 = f32[2,256,256]{2,1,0:T(8,128)} copy(f32[2,256,256]{2,1,0:T(8,128)S(1)} %update.1) | data formatting | bytes 1048576
